TPU v7x, 32 devices: a whole 2x2x4 slice. The times are simulated.
32 devices in a mesh: gx: 4 (over z), gy: 4 (over y, x), gz: 2 (over core).
Axes of the slice: x: 2, y: 2, z: 4, core: 2. Of those that a mesh axis runs over, the one named last changes fastest.
Arguments:
- panel: float32 [8192, 4096], P(('gx', 'gy', 'gz'))
- treat_start: int32 [8192], P(('gx', 'gy', 'gz')), may hold values from 1024 to 4096
- loading_init: float32 [64, 8192], P(None, ('gx', 'gy', 'gz'))
- factor_init: float32 [64, 4096], P(None, ('gx', 'gy', 'gz'))
- unit_init: float32 [8192], P(('gx', 'gy', 'gz'))
- day_init: float32 [4096], replicated
Outputs:
- loading_out: float32 [64, 8192], P(None, ('gx', 'gy', 'gz'))
- factor_out: float32 [64, 4096], P(None, ('gx', 'gy', 'gz'))
- unit_out: float32 [8192], P(('gx', 'gy', 'gz'))
- day_out: float32 [4096], replicated
Inputs may be any that keep to these rules, and one draw needn't show every extreme that they name: A unit is treated from day treat_start on; 4096 means never treated.
All inputs are finite; a program needn't handle non-finite values.
Results may differ from a plain program's by a relative error of at most 0.0001.
Values sent between devices are 32-bit elements; how exact they have to be, the bound alone decides.
A program may use at most 64 MiB of HBM per device.

v0:
```python
import jax
import jax.numpy as jnp
from jax import lax
from jax.sharding import PartitionSpec as P

SWEEPS = 2
RIDGE = 1.0


def solve_spd(matrix, right):
    lower = jnp.linalg.cholesky(matrix)
    middle = lax.linalg.triangular_solve(lower, right, left_side=True, lower=True)
    return lax.linalg.triangular_solve(lower, middle, left_side=True, lower=True, transpose_a=True)


def contract_first(left, right):
    return lax.dot_general(
        left,
        right,
        (((0,), (0,)), ((), ())),
        precision=lax.Precision.HIGHEST,
        preferred_element_type=jnp.float32,
    )


def contract_last(left, right):
    return lax.dot_general(
        left,
        right,
        (((1,), (1,)), ((), ())),
        precision=lax.Precision.HIGHEST,
        preferred_element_type=jnp.float32,
    )


def body(panel, treat_start, loading_init, factor_init, unit_init, day_init):
    unit_rows, total_days = panel.shape
    devices = lax.axis_size(("gx", "gy", "gz"))
    all_units = unit_rows * devices
    slice_days = factor_init.shape[1]
    rank = loading_init.shape[0]
    ridge_eye = jnp.eye(rank, dtype=jnp.float32) * RIDGE
    observed = lax.broadcasted_iota(jnp.int32, (unit_rows, total_days), 1) < treat_start[:, None]
    loading = loading_init
    unit_eff = unit_init
    day_eff = day_init
    factors = None
    owned_factors = factor_init
    for sweep_index in range(SWEEPS):
        unit_gram = lax.psum(contract_last(loading, loading), ("gx", "gy", "gz"))
        if sweep_index == 0:
            fitted = contract_first(
                loading, lax.all_gather(factor_init, ("gx", "gy", "gz"), axis=1, tiled=True)
            )
        else:
            fitted = contract_first(loading, factors)
        imputed = jnp.where(observed, panel, unit_eff[:, None] + day_eff[None, :] + fitted)
        without = imputed - fitted
        day_part = jnp.sum(without, 0)
        row_sums = jnp.sum(without, 1)
        resid = None
        day_sums = lax.psum(day_part, ("gx", "gy", "gz"))
        grand = jnp.sum(day_sums) / (all_units * total_days)
        day_eff = day_sums / all_units - grand
        unit_eff = row_sums / total_days - grand
        resid = imputed - unit_eff[:, None] - day_eff[None, :]
        payload = jnp.dot(loading, resid, precision=lax.Precision.HIGHEST)
        summed = lax.psum(payload, ("gx", "gy", "gz"))
        factors = solve_spd(unit_gram + ridge_eye, summed)
        owned_factors = lax.dynamic_slice_in_dim(
            factors, lax.axis_index(("gx", "gy", "gz")) * slice_days, slice_days, 1
        )
        factor_gram = jnp.dot(factors, factors.T, precision=lax.Precision.HIGHEST)
        loading = solve_spd(factor_gram + ridge_eye, contract_last(factors, resid))
    return (loading, owned_factors, unit_eff, day_eff)


def solution(mesh):
    return jax.shard_map(
        body,
        mesh=mesh,
        in_specs=(
            P(("gx", "gy", "gz"), None),
            P(("gx", "gy", "gz")),
            P(None, ("gx", "gy", "gz")),
            P(None, ("gx", "gy", "gz")),
            P(("gx", "gy", "gz")),
            P(),
        ),
        out_specs=(
            P(None, ("gx", "gy", "gz")),
            P(None, ("gx", "gy", "gz")),
            P(("gx", "gy", "gz")),
            P(),
        ),
        check_vma=False,
    )
```

profile of v0, /device:TPU:0, one launch (start us, length us, event | category | flops | bytes accessed | tf_op | source)
XLA Modules:
  0.0 507.0 jit_solution(17631101533937465551)
XLA Ops:
  7.2 0.7 all-gather.2.cloned.1.call-update
  8.3 57.7 %all-gather.2.cloned.1.call-done = f32[64,4096]{1,0:T(8,128)} async-done(((f32[64,128]{1,0:T(8,128)}), f32[64,4096]{1,0:T(8,128)}) %all-gather.2.cloned.1.call-update) | async-done | bytes 1048592 | tf_op jit(solution)/shard_map/all_gather | solution.py:53
  65.9 7.9 %subtract_reduce_fusion.3 = (f32[256]{0:T(256)S(1)}, f32[4096]{0:T(1024)S(1)}, f32[256,4096]{1,0:T(8,128)}) fusion(f32[256,4096]{1,0:T(8,128)} %param.15, f32[4096]{0:T(1024)} %param.20, f32[256]{0:T(256)} %param.19, s32[256]{0:T(256)} %param.16, f32[64,256]{1,0:T(8,128)S(1)} %copy-done, f32[64,4096]{1,0:T(8,128)} %all-gather.2.cloned.1.call-done), kind=kOutput, calls=%fused_computation.20 | convolution fusion | flops 812642048 | bytes 9538560 | tf_op jit(solution)/shard_map/dot_general | solution.py:17
  73.8 40.5 %all-reduce.1 = (f32[4096]{0:T(1024)S(1)}, f32[64,64]{0,1:T(8,128)S(1)}) all-reduce(f32[4096]{0:T(1024)S(1)} %get-tuple-element.12, f32[64,64]{0,1:T(8,128)S(1)} %fusion.41), channel_id=1, replica_groups=mesh['gx'=4,'gy'=4,'gz'=2] {'gx','gy','gz'}, use_global_device_ids=true, to_apply=%region_5.0 | all-reduce | flops 8192 | bytes 65536 | tf_op jit(solution)/shard_map/psum | solution.py:62
  115.6 12.0 %convolution_bitcast_fusion = f32[64,4096]{0,1:T(8,128)} fusion(f32[64,256]{1,0:T(8,128)S(1)} %copy-done, f32[4096]{0:T(1024)S(1)} %multiply_subtract_fusion.1, f32[256]{0:T(256)S(1)} %multiply_subtract_fusion.3, f32[256,4096]{1,0:T(8,128)} %param.15, f32[256,4096]{1,0:T(8,128)} %get-tuple-element.17, f32[4096]{0:T(1024)S(1)} %copy-done.3, ...), kind=kOutput, calls=%fused_computation | convolution fusion | flops 811597824 | bytes 9538560 | tf_op jit(solution)/shard_map/dot_general | solution.py:67
  127.6 10.1 %all-reduce.7.cloned.1.call-start = ((), (), s32[]{:S(2)}) async-start(), calls=%async_computation.2 | async-start | bytes 2097152 | tf_op jit(solution)/shard_map/psum | solution.py:68
  137.8 5.8 %cholesky.74 = f32[64,64]{1,0:T(8,128)S(1)} custom-call(f32[64,64]{1,0:T(8,128)S(1)} %fusion.34), custom_call_target="Cholesky" | custom-call | tf_op jit(solution)/shard_map/jit(cholesky)/cholesky | solution.py:11
  144.3 0.7 fusion.11
  145.0 4.9 custom-call.19
  149.9 111.7 %all-reduce.5.cloned.1.call-done = f32[64,4096]{0,1:T(8,128)} async-done(((f32[64,4096]{0,1:T(8,128)}), f32[64,4096]{0,1:T(8,128)}) %all-reduce.5.cloned.1.call-update) | async-done | bytes 1048592 | tf_op jit(solution)/shard_map/psum | solution.py:68
  261.6 4.1 fusion.30
  265.7 1.0 fusion.32
  266.7 1.0 convolution_add_fusion.1
  267.7 6.6 %fusion = f32[64,256]{1,0:T(8,128)S(1)} fusion(f32[64,4096]{1,0:T(8,128)S(1)} %fusion.32, f32[4096]{0:T(1024)S(1)} %multiply_subtract_fusion.1, f32[256]{0:T(256)S(1)} %multiply_subtract_fusion.3, f32[256,4096]{1,0:T(8,128)S(1)} %copy-done.1, f32[256,4096]{1,0:T(8,128)} %get-tuple-element.17, f32[4096]{0:T(1024)S(1)} %copy-done.3, f32[256]{0:T(256)S(1)} %copy-done.6, ...), kind=kOutput, calls=%fused_computation.6 | convolution fusion | flops 811597824 | bytes 9538560 | tf_op jit(solution)/shard_map/dot_general | solution.py:27
  274.4 5.8 %cholesky.85 = f32[64,64]{1,0:T(8,128)S(1)} custom-call(f32[64,64]{1,0:T(8,128)S(1)} %fusion.29), custom_call_target="Cholesky" | custom-call | tf_op jit(solution)/shard_map/jit(cholesky)/cholesky | solution.py:11
  281.0 0.7 fusion.12
  281.6 4.9 custom-call.21
  287.0 7.7 %subtract_reduce_fusion.1 = (f32[256]{0:T(256)S(1)}, f32[4096]{0:T(1024)S(1)}, f32[256,4096]{1,0:T(8,128)}) fusion(f32[256,4096]{1,0:T(8,128)} %param.15, f32[4096]{0:T(1024)S(1)} %multiply_subtract_fusion.1, f32[256]{0:T(256)S(1)} %multiply_subtract_fusion.3, s32[256]{0:T(256)S(1)} %copy-done.5, f32[64,256]{1,0:T(8,128)S(1)} %fusion.27, ...), kind=kOutput, calls=%fused_computation.18 | convolution fusion | flops 812642048 | bytes 9538560 | tf_op jit(solution)/shard_map/dot_general | solution.py:17
  294.9 39.5 %all-reduce = (f32[4096]{0:T(1024)S(1)}, f32[64,64]{0,1:T(8,128)S(1)}) all-reduce(f32[4096]{0:T(1024)S(1)} %get-tuple-element.10, f32[64,64]{0,1:T(8,128)S(1)} %fusion.42), channel_id=1, replica_groups=mesh['gx'=4,'gy'=4,'gz'=2] {'gx','gy','gz'}, use_global_device_ids=true, to_apply=%region_11.17 | all-reduce | flops 8192 | bytes 65536 | tf_op jit(solution)/shard_map/psum | solution.py:62
  335.9 8.1 %fusion.2 = f32[64,4096]{1,0:T(8,128)} fusion(f32[64,256]{1,0:T(8,128)S(1)} %fusion.27, f32[4096]{0:T(1024)S(1)} %multiply_subtract_fusion, f32[256]{0:T(256)S(1)} %multiply_subtract_fusion.2, f32[256,4096]{1,0:T(8,128)} %param.15, f32[256,4096]{1,0:T(8,128)} %get-tuple-element.18, f32[4096]{0:T(1024)S(1)} %multiply_subtract_fusion.1, ...), kind=kOutput, calls=%fused_computation.8 | convolution fusion | flops 811597824 | bytes 9538560 | tf_op jit(solution)/shard_map/dot_general | solution.py:67
  344.0 5.8 %cholesky.96 = f32[64,64]{1,0:T(8,128)S(1)} custom-call(f32[64,64]{1,0:T(8,128)S(1)} %fusion.24), custom_call_target="Cholesky" | custom-call | tf_op jit(solution)/shard_map/jit(cholesky)/cholesky | solution.py:11
  350.5 0.7 fusion.13
  351.2 4.9 custom-call.23
  356.1 119.0 %all-reduce.7.cloned.1.call-done = f32[64,4096]{1,0:T(8,128)} async-done(((f32[64,4096]{1,0:T(8,128)}), f32[64,4096]{1,0:T(8,128)}) %all-reduce.7.cloned.1.call-update) | async-done | bytes 1048592 | tf_op jit(solution)/shard_map/psum | solution.py:68
  475.1 2.4 fusion.20
  477.5 1.0 fusion.22
  478.5 1.0 convolution_add_fusion
  479.5 6.6 %fusion.1 = f32[64,256]{1,0:T(8,128)S(1)} fusion(f32[64,4096]{1,0:T(8,128)S(1)} %fusion.22, f32[4096]{0:T(1024)S(1)} %multiply_subtract_fusion, f32[256]{0:T(256)S(1)} %multiply_subtract_fusion.2, f32[256,4096]{1,0:T(8,128)S(1)} %copy-done.2, f32[256,4096]{1,0:T(8,128)} %get-tuple-element.18, f32[4096]{0:T(1024)S(1)} %multiply_subtract_fusion.1, ...), kind=kOutput, calls=%fused_computation.7 | convolution fusion | flops 811597824 | bytes 9538560 | tf_op jit(solution)/shard_map/dot_general | solution.py:27
  486.2 5.8 %cholesky.107 = f32[64,64]{1,0:T(8,128)S(1)} custom-call(f32[64,64]{1,0:T(8,128)S(1)} %fusion.19), custom_call_target="Cholesky" | custom-call | tf_op jit(solution)/shard_map/jit(cholesky)/cholesky | solution.py:11
  492.8 0.7 fusion.14
  493.4 4.9 custom-call.25
  498.6 0.8 fusion.17
  (50 shorter events, 6.3 us)
Async XLA Ops:
  7.2 0.8 copy-start
  7.2 58.7 %all-gather.2.cloned.1.call-start = ((), (), s32[]{:S(2)}) async-start(), calls=%async_computation | async-start | bytes 1081344 | tf_op jit(solution)/shard_map/all_gather | solution.py:53
  7.9 253.7 %all-reduce.5.cloned.1.call-start = ((), (), s32[]{:S(2)}) async-start(), calls=%async_computation.1 | async-start | bytes 4194304 | tf_op jit(solution)/shard_map/psum | solution.py:68
  8.2 107.4 %copy-start.3 = (f32[4096]{0:T(1024)S(1)}, f32[4096]{0:T(1024)}, u32[]{:S(2)}) copy-start(f32[4096]{0:T(1024)} %param.20) | copy-start | bytes 49156
  8.2 107.4 %copy-start.5 = (s32[256]{0:T(256)S(1)}, s32[256]{0:T(256)}, u32[]{:S(2)}) copy-start(s32[256]{0:T(256)} %param.16) | copy-start | bytes 3076
  8.2 107.4 %copy-start.6 = (f32[256]{0:T(256)S(1)}, f32[256]{0:T(256)}, u32[]{:S(2)}) copy-start(f32[256]{0:T(256)} %param.19) | copy-start | bytes 3076
  127.6 347.5 %all-reduce.7.cloned.1.call-start = ((), (), s32[]{:S(2)}) async-start(), calls=%async_computation.2 | async-start | bytes 2097152 | tf_op jit(solution)/shard_map/psum | solution.py:68
  261.6 6.1 %copy-start.1 = (f32[256,4096]{1,0:T(8,128)S(1)}, f32[256,4096]{1,0:T(8,128)}, u32[]{:S(2)}) copy-start(f32[256,4096]{1,0:T(8,128)} %param.15) | copy-start | bytes 12582916
  335.8 143.6 %copy-start.4 = (f32[4096]{0:T(1024)}, f32[4096]{0:T(1024)S(1)}, u32[]{:S(2)}) copy-start(f32[4096]{0:T(1024)S(1)} %multiply_subtract_fusion) | copy-start | bytes 49156
  335.9 143.6 %copy-start.7 = (f32[256]{0:T(256)}, f32[256]{0:T(256)S(1)}, u32[]{:S(2)}) copy-start(f32[256]{0:T(256)S(1)} %multiply_subtract_fusion.2) | copy-start | bytes 3076
  475.1 4.4 copy-start.2
Sparse Core Ops, SparseCore 0:
  10.9 55.0 all-gather.1
  127.7 133.8 all-reduce.4
  344.1 130.8 all-reduce.6
where the time goes:
time: 515 us; the launch traced here: 507 us
  waiting for transfers between devices  289 us (56%)
  blocking collectives  80 us (16%)
  matrix products  61.4 us (12%)
  other arithmetic  49.6 us (10%)
  between operations  15.8 us (3%)
  starting transfers between devices  10.2 us (2%)
    psum x2, waiting for transfers between devices, body(): summed = lax.psum(payload, ('gx', 'gy', 'gz'))  231 us
    psum x2, blocking collectives, body(): day_sums = lax.psum(day_part, ('gx', 'gy', 'gz'))  80 us
    all_gather x1, waiting for transfers between devices, body(): lax.all_gather(factor_init, ('gx', 'gy', 'gz'), axis=1, tiled=True)  57.7 us
    another operation x12, other arithmetic, solve_spd(): lower = jnp.linalg.cholesky(matrix)  26.1 us
    another operation x8, other arithmetic, solve_spd(): lax.linalg.triangular_solve(lower, middle, left_side=True, lower=True, tr...  22.2 us
    dot_general x2, matrix products, body(): payload = jnp.dot(loading, resid, precision=lax.Precision.HIGHEST)  20 us
    dot_general x2, matrix products, contract_first(): lax.dot_general(left, right, (((0,), (0,)), ((), ())), precision=lax.Prec...  15.6 us
    dot_general x4, matrix products, contract_last(): lax.dot_general(left, right, (((1,), (1,)), ((), ())), precision=lax.Prec...  13.7 us
  transfers between devices with their start and end apart: 3, of which 3 were waited for; matrix products, arithmetic and copies ran while one was open for 5% of the time, Pallas kernels for 0%

commit v1 on v0

--- a/solution.py
+++ b/solution.py
@@ -5,6 +5,10 @@
 
 SWEEPS = 2
 RIDGE = 1.0
+
+
+def edit_grid_up(z, row_axis, axis_key):
+    return jax.lax.psum(jax.lax.psum(z, row_axis), axis_key)
 
 
 def solve_spd(matrix, right):
@@ -59,7 +63,7 @@
         day_part = jnp.sum(without, 0)
         row_sums = jnp.sum(without, 1)
         resid = None
-        day_sums = lax.psum(day_part, ("gx", "gy", "gz"))
+        day_sums = edit_grid_up(day_part, row_axis=("gy", "gz"), axis_key="gx")
         grand = jnp.sum(day_sums) / (all_units * total_days)
         day_eff = day_sums / all_units - grand
         unit_eff = row_sums / total_days - grand

time: 515 us -> 552 us (1.072)
  blocking collectives: 80 us -> 164 us
  waiting for transfers between devices: 289 us -> 241 us
    psum x2 -> x6, blocking collectives: 80 us -> 164 us  [the longest x4 82.6 us: edit_grid_up(): return jax.lax.psum(jax.lax.psum(z, row_axis), axis_key)]
    all_gather x1, waiting for transfers between devices: 57.7 us -> 15.5 us  [body(): lax.all_gather(factor_init, ('gx', 'gy', 'gz'), axis=1, tiled=True)]
    psum x2, waiting for transfers between devices: 231 us -> 225 us  [body(): summed = lax.psum(payload, ('gx', 'gy', 'gz'))]
where the time goes in v1:
time: 552 us; the launch traced here: 543 us
  waiting for transfers between devices  241 us (44%)
  blocking collectives  164 us (30%)
  matrix products  61.4 us (11%)
  other arithmetic  49.6 us (9%)
  between operations  15.8 us (3%)
  starting transfers between devices  10.5 us (2%)
    psum x2, waiting for transfers between devices, body(): summed = lax.psum(payload, ('gx', 'gy', 'gz'))  225 us
    psum x4, blocking collectives, edit_grid_up(): return jax.lax.psum(jax.lax.psum(z, row_axis), axis_key)  82.6 us
    psum x2, blocking collectives, body(): unit_gram = lax.psum(contract_last(loading, loading), ('gx', 'gy', 'gz'))  81.1 us
    another operation x12, other arithmetic, solve_spd(): lower = jnp.linalg.cholesky(matrix)  26.1 us
    another operation x8, other arithmetic, solve_spd(): lax.linalg.triangular_solve(lower, middle, left_side=True, lower=True, tr...  22.2 us
    dot_general x2, matrix products, body(): payload = jnp.dot(loading, resid, precision=lax.Precision.HIGHEST)  20 us
    dot_general x2, matrix products, contract_first(): lax.dot_general(left, right, (((0,), (0,)), ((), ())), precision=lax.Prec...  15.6 us
    all_gather x1, waiting for transfers between devices, body(): lax.all_gather(factor_init, ('gx', 'gy', 'gz'), axis=1, tiled=True)  15.5 us
  transfers between devices with their start and end apart: 3, of which 3 were waited for; matrix products, arithmetic and copies ran while one was open for 5% of the time, Pallas kernels for 0%

profile of v1, /device:TPU:0, one launch (start us, length us, event | category | flops | bytes accessed | tf_op | source)
XLA Modules:
  0.0 543.1 jit_solution(18379160564300455933)
XLA Ops:
  7.2 0.7 all-gather.2.cloned.1.call-update
  8.2 42.1 %psum.56 = f32[64,64]{0,1:T(8,128)S(1)} all-reduce(f32[64,64]{0,1:T(8,128)S(1)} %fusion.41), channel_id=1, replica_groups=mesh['gx'=4,'gy'=4,'gz'=2] {'gx','gy','gz'}, use_global_device_ids=true, to_apply=%region_0.0 | all-reduce | flops 4096 | bytes 32768 | tf_op jit(solution)/shard_map/psum | solution.py:54
  50.5 15.5 %all-gather.2.cloned.1.call-done = f32[64,4096]{1,0:T(8,128)} async-done(((f32[64,128]{1,0:T(8,128)}), f32[64,4096]{1,0:T(8,128)}) %all-gather.2.cloned.1.call-update) | async-done | bytes 1048592 | tf_op jit(solution)/shard_map/all_gather | solution.py:57
  66.0 7.9 %subtract_reduce_fusion.3 = (f32[256]{0:T(256)S(1)}, f32[4096]{0:T(1024)S(1)}, f32[256,4096]{1,0:T(8,128)}) fusion(f32[256,4096]{1,0:T(8,128)} %param.15, f32[4096]{0:T(1024)} %param.20, f32[256]{0:T(256)} %param.19, s32[256]{0:T(256)} %param.16, f32[64,256]{1,0:T(8,128)S(1)} %copy-done, f32[64,4096]{1,0:T(8,128)} %all-gather.2.cloned.1.call-done), kind=kOutput, calls=%fused_computation.20 | convolution fusion | flops 812642048 | bytes 9538560 | tf_op jit(solution)/shard_map/dot_general | solution.py:21
  73.9 24.4 %psum.57 = f32[4096]{0:T(1024)S(1)} all-reduce(f32[4096]{0:T(1024)S(1)} %get-tuple-element.12), channel_id=1, replica_groups=mesh['gx'=4,'gy'=4,'gz'=2] {'gy','gz'}, use_global_device_ids=true, to_apply=%region_5.0 | all-reduce | flops 4096 | bytes 32768 | tf_op jit(solution)/shard_map/psum | solution.py:11
  98.4 17.4 %psum.58 = f32[4096]{0:T(1024)S(1)} all-reduce(f32[4096]{0:T(1024)S(1)} %psum.57), channel_id=1, replica_groups=mesh['gx'=4,'gy'=4,'gz'=2] {'gx'}, use_global_device_ids=true, to_apply=%region_6.0 | all-reduce | flops 4096 | bytes 32768 | tf_op jit(solution)/shard_map/psum | solution.py:11
  117.1 12.0 %convolution_bitcast_fusion = f32[64,4096]{0,1:T(8,128)} fusion(f32[64,256]{1,0:T(8,128)S(1)} %copy-done, f32[4096]{0:T(1024)S(1)} %multiply_subtract_fusion.1, f32[256]{0:T(256)S(1)} %multiply_subtract_fusion.3, f32[256,4096]{1,0:T(8,128)} %param.15, f32[256,4096]{1,0:T(8,128)} %get-tuple-element.13, f32[4096]{0:T(1024)S(1)} %copy-done.3, ...), kind=kOutput, calls=%fused_computation | convolution fusion | flops 811597824 | bytes 9538560 | tf_op jit(solution)/shard_map/dot_general | solution.py:71
  129.1 10.4 %all-reduce.5.cloned.1.call-start = ((), (), s32[]{:S(2)}) async-start(), calls=%async_computation.2 | async-start | bytes 2097152 | tf_op jit(solution)/shard_map/psum | solution.py:72
  139.5 5.8 %cholesky.74 = f32[64,64]{1,0:T(8,128)S(1)} custom-call(f32[64,64]{1,0:T(8,128)S(1)} %fusion.34), custom_call_target="Cholesky" | custom-call | tf_op jit(solution)/shard_map/jit(cholesky)/cholesky | solution.py:15
  146.7 4.9 custom-call.19
  151.6 108.8 %all-reduce.3.cloned.1.call-done = f32[64,4096]{0,1:T(8,128)} async-done(((f32[64,4096]{0,1:T(8,128)}), f32[64,4096]{0,1:T(8,128)}) %all-reduce.3.cloned.1.call-update) | async-done | bytes 1048592 | tf_op jit(solution)/shard_map/psum | solution.py:72
  260.4 4.1 fusion.30
  264.4 1.0 fusion.32
  265.4 1.0 convolution_add_fusion.1
  266.4 6.6 %fusion = f32[64,256]{1,0:T(8,128)S(1)} fusion(f32[64,4096]{1,0:T(8,128)S(1)} %fusion.32, f32[4096]{0:T(1024)S(1)} %multiply_subtract_fusion.1, f32[256]{0:T(256)S(1)} %multiply_subtract_fusion.3, f32[256,4096]{1,0:T(8,128)S(1)} %copy-done.1, f32[256,4096]{1,0:T(8,128)} %get-tuple-element.13, f32[4096]{0:T(1024)S(1)} %copy-done.3, f32[256]{0:T(256)S(1)} %copy-done.6, ...), kind=kOutput, calls=%fused_computation.6 | convolution fusion | flops 811597824 | bytes 9538560 | tf_op jit(solution)/shard_map/dot_general | solution.py:31
  273.2 5.8 %cholesky.85 = f32[64,64]{1,0:T(8,128)S(1)} custom-call(f32[64,64]{1,0:T(8,128)S(1)} %fusion.29), custom_call_target="Cholesky" | custom-call | tf_op jit(solution)/shard_map/jit(cholesky)/cholesky | solution.py:15
  280.4 4.9 custom-call.21
  286.0 7.7 %subtract_reduce_fusion.1 = (f32[256]{0:T(256)S(1)}, f32[4096]{0:T(1024)S(1)}, f32[256,4096]{1,0:T(8,128)}) fusion(f32[256,4096]{1,0:T(8,128)} %param.15, f32[4096]{0:T(1024)S(1)} %multiply_subtract_fusion.1, f32[256]{0:T(256)S(1)} %multiply_subtract_fusion.3, s32[256]{0:T(256)S(1)} %copy-done.5, f32[64,256]{1,0:T(8,128)S(1)} %fusion.27, ...), kind=kOutput, calls=%fused_computation.18 | convolution fusion | flops 812642048 | bytes 9538560 | tf_op jit(solution)/shard_map/dot_general | solution.py:21
  293.7 39.0 %psum.60 = f32[64,64]{0,1:T(8,128)S(1)} all-reduce(f32[64,64]{0,1:T(8,128)S(1)} %fusion.42), channel_id=1, replica_groups=mesh['gx'=4,'gy'=4,'gz'=2] {'gx','gy','gz'}, use_global_device_ids=true, to_apply=%region_9.15 | all-reduce | flops 4096 | bytes 32768 | tf_op jit(solution)/shard_map/psum | solution.py:54
  332.8 23.1 %psum.61 = f32[4096]{0:T(1024)S(1)} all-reduce(f32[4096]{0:T(1024)S(1)} %get-tuple-element.10), channel_id=1, replica_groups=mesh['gx'=4,'gy'=4,'gz'=2] {'gy','gz'}, use_global_device_ids=true, to_apply=%region_12.18 | all-reduce | flops 4096 | bytes 32768 | tf_op jit(solution)/shard_map/psum | solution.py:11
  355.9 17.6 %psum.62 = f32[4096]{0:T(1024)S(1)} all-reduce(f32[4096]{0:T(1024)S(1)} %psum.61), channel_id=1, replica_groups=mesh['gx'=4,'gy'=4,'gz'=2] {'gx'}, use_global_device_ids=true, to_apply=%region_13.19 | all-reduce | flops 4096 | bytes 32768 | tf_op jit(solution)/shard_map/psum | solution.py:11
  374.8 8.1 %fusion.2 = f32[64,4096]{1,0:T(8,128)} fusion(f32[64,256]{1,0:T(8,128)S(1)} %fusion.27, f32[4096]{0:T(1024)S(1)} %multiply_subtract_fusion, f32[256]{0:T(256)S(1)} %multiply_subtract_fusion.2, f32[256,4096]{1,0:T(8,128)} %param.15, f32[256,4096]{1,0:T(8,128)} %get-tuple-element.14, f32[4096]{0:T(1024)S(1)} %multiply_subtract_fusion.1, ...), kind=kOutput, calls=%fused_computation.8 | convolution fusion | flops 811597824 | bytes 9538560 | tf_op jit(solution)/shard_map/dot_general | solution.py:71
  382.9 5.8 %cholesky.96 = f32[64,64]{1,0:T(8,128)S(1)} custom-call(f32[64,64]{1,0:T(8,128)S(1)} %fusion.24), custom_call_target="Cholesky" | custom-call | tf_op jit(solution)/shard_map/jit(cholesky)/cholesky | solution.py:15
  390.1 4.9 custom-call.23
  395.0 116.2 %all-reduce.5.cloned.1.call-done = f32[64,4096]{1,0:T(8,128)} async-done(((f32[64,4096]{1,0:T(8,128)}), f32[64,4096]{1,0:T(8,128)}) %all-reduce.5.cloned.1.call-update) | async-done | bytes 1048592 | tf_op jit(solution)/shard_map/psum | solution.py:72
  511.2 2.4 fusion.20
  513.6 1.0 fusion.22
  514.7 1.0 convolution_add_fusion
  515.7 6.6 %fusion.1 = f32[64,256]{1,0:T(8,128)S(1)} fusion(f32[64,4096]{1,0:T(8,128)S(1)} %fusion.22, f32[4096]{0:T(1024)S(1)} %multiply_subtract_fusion, f32[256]{0:T(256)S(1)} %multiply_subtract_fusion.2, f32[256,4096]{1,0:T(8,128)S(1)} %copy-done.2, f32[256,4096]{1,0:T(8,128)} %get-tuple-element.14, f32[4096]{0:T(1024)S(1)} %multiply_subtract_fusion.1, ...), kind=kOutput, calls=%fused_computation.7 | convolution fusion | flops 811597824 | bytes 9538560 | tf_op jit(solution)/shard_map/dot_general | solution.py:31
  522.4 5.8 %cholesky.107 = f32[64,64]{1,0:T(8,128)S(1)} custom-call(f32[64,64]{1,0:T(8,128)S(1)} %fusion.19), custom_call_target="Cholesky" | custom-call | tf_op jit(solution)/shard_map/jit(cholesky)/cholesky | solution.py:15
  529.6 4.9 custom-call.25
  534.8 0.8 fusion.17
  (54 shorter events, 8.9 us)
Async XLA Ops:
  7.2 0.8 copy-start
  7.2 58.8 %all-gather.2.cloned.1.call-start = ((), (), s32[]{:S(2)}) async-start(), calls=%async_computation | async-start | bytes 1081344 | tf_op jit(solution)/shard_map/all_gather | solution.py:57
  7.9 252.4 %all-reduce.3.cloned.1.call-start = ((), (), s32[]{:S(2)}) async-start(), calls=%async_computation.1 | async-start | bytes 4194304 | tf_op jit(solution)/shard_map/psum | solution.py:72
  50.5 66.6 %copy-start.3 = (f32[4096]{0:T(1024)S(1)}, f32[4096]{0:T(1024)}, u32[]{:S(2)}) copy-start(f32[4096]{0:T(1024)} %param.20) | copy-start | bytes 49156
  50.5 66.6 %copy-start.5 = (s32[256]{0:T(256)S(1)}, s32[256]{0:T(256)}, u32[]{:S(2)}) copy-start(s32[256]{0:T(256)} %param.16) | copy-start | bytes 3076
  50.5 66.6 %copy-start.6 = (f32[256]{0:T(256)S(1)}, f32[256]{0:T(256)}, u32[]{:S(2)}) copy-start(f32[256]{0:T(256)} %param.19) | copy-start | bytes 3076
  129.1 382.1 %all-reduce.5.cloned.1.call-start = ((), (), s32[]{:S(2)}) async-start(), calls=%async_computation.2 | async-start | bytes 2097152 | tf_op jit(solution)/shard_map/psum | solution.py:72
  260.4 6.1 %copy-start.1 = (f32[256,4096]{1,0:T(8,128)S(1)}, f32[256,4096]{1,0:T(8,128)}, u32[]{:S(2)}) copy-start(f32[256,4096]{1,0:T(8,128)} %param.15) | copy-start | bytes 12582916
  374.8 140.9 %copy-start.4 = (f32[4096]{0:T(1024)}, f32[4096]{0:T(1024)S(1)}, u32[]{:S(2)}) copy-start(f32[4096]{0:T(1024)S(1)} %multiply_subtract_fusion) | copy-start | bytes 49156
  374.8 140.9 %copy-start.7 = (f32[256]{0:T(256)}, f32[256]{0:T(256)S(1)}, u32[]{:S(2)}) copy-start(f32[256]{0:T(256)S(1)} %multiply_subtract_fusion.2) | copy-start | bytes 3076
  511.2 4.5 copy-start.2
Sparse Core Ops, SparseCore 0:
  10.9 55.1 all-gather.1
  129.2 131.0 all-reduce.2
  383.0 128.1 all-reduce.4
